TPU v7x, 32 devices: a whole 2x2x4 slice. The times are simulated.
32 devices in a mesh: gz: 4 (over z), gy: 4 (over y, x), gx: 2 (over core).
Axes of the slice: x: 2, y: 2, z: 4, core: 2. Of those that a mesh axis runs over, the one named last changes fastest.
Arguments:
- right_side: float32 [32, 64, 256], P('gz', 'gy', 'gx'), may hold values from -128 to 128
- diagonal: float32 [32, 64, 256], P('gz', 'gy', 'gx'), may hold values from 0.05 to 1
Outputs:
- solution_field: float32 [32, 64, 256], P('gz', 'gy', 'gx')
- residual: float32 [32, 64, 256], P('gz', 'gy', 'gx')
All inputs are finite; a program needn't handle non-finite values.
Results may differ from a plain program's by a relative error of at most 0.03.
Values sent between devices are 32-bit elements.
A program may use at most 64 MiB of HBM per device.

v0:
```python
import jax
import jax.numpy as jnp
import numpy as np
from jax import lax
from jax.sharding import PartitionSpec as P

S = 6
OUTER = 5


center_shift = 19.0
half_width = 19.0


def extended_2(block, sides, width, periodic):
    for axis, dim in sides:
        count = lax.axis_size(axis)
        forward = [(i, i + 1) for i in range(count - 1)]
        if periodic:
            forward.append((count - 1, 0))
        backward = [(target, source) for source, target in forward]
        low = lax.ppermute(
            lax.slice_in_dim(block, block.shape[dim] - width, None, axis=dim), axis, forward
        )
        high = lax.ppermute(lax.slice_in_dim(block, 0, width, axis=dim), axis, backward)
        block = jnp.concatenate([low, block, high], axis=dim)
    return block


def apply_operator(padded, diagonal):
    extent_z = padded.shape[-3] - 2
    extent_y = padded.shape[-2] - 2
    extent_x = padded.shape[-1] - 2
    running = jnp.zeros(padded[..., 1:-1, 1:-1, 1:-1].shape, jnp.float32)
    for along_z in range(3):
        for along_y in range(3):
            for along_x in range(3):
                if along_z == 1 and along_y == 1 and (along_x == 1):
                    continue
                running = (
                    running
                    + padded[
                        ...,
                        along_z : along_z + extent_z,
                        along_y : along_y + extent_y,
                        along_x : along_x + extent_x,
                    ]
                )
    return (26.0 + diagonal) * padded[..., 1:-1, 1:-1, 1:-1] - running


def chebyshev_next(images, current, previous):
    scaled = (images - center_shift * current) / half_width
    if previous is None:
        return scaled
    return 2.0 * scaled - previous


def basis_change():
    columns = 2 * S + 1
    matrix = np.zeros((columns, columns), np.float32)
    for offset, length in ((0, S), (S + 1, S - 1)):
        for degree in range(length):
            matrix[offset + degree, offset + degree] = center_shift
            if degree == 0:
                matrix[offset + 1, offset] = half_width
            else:
                matrix[offset + degree + 1, offset + degree] = 0.5 * half_width
                matrix[offset + degree - 1, offset + degree] = 0.5 * half_width
    return matrix


def coefficients(gram_matrix):
    columns = 2 * S + 1
    change = jnp.asarray(basis_change(), dtype=jnp.float32)
    identity = jnp.eye(columns, dtype=jnp.float32)
    dir_coeff = identity[0]
    res_coeff = identity[S + 1]
    sol_coeff = jnp.zeros((columns,), jnp.float32)
    for degree in range(S):
        moved = jnp.dot(change, dir_coeff, precision=lax.Precision.HIGHEST)
        norm_now = jnp.dot(
            res_coeff,
            jnp.dot(gram_matrix, res_coeff, precision=lax.Precision.HIGHEST),
            precision=lax.Precision.HIGHEST,
        )
        curvature = jnp.dot(
            dir_coeff,
            jnp.dot(gram_matrix, moved, precision=lax.Precision.HIGHEST),
            precision=lax.Precision.HIGHEST,
        )
        step_len = norm_now / curvature
        sol_coeff = sol_coeff + step_len * dir_coeff
        res_next = res_coeff - step_len * moved
        norm_next = jnp.dot(
            res_next,
            jnp.dot(gram_matrix, res_next, precision=lax.Precision.HIGHEST),
            precision=lax.Precision.HIGHEST,
        )
        dir_coeff = res_next + norm_next / norm_now * dir_coeff
        res_coeff = res_next
    return (sol_coeff, res_coeff, dir_coeff)


def combine(coeff, basis_set):
    return jnp.tensordot(coeff, basis_set, axes=1, precision=lax.Precision.HIGHEST)


def crop_margin(values, amount):
    if amount == 0:
        return values
    return values[..., amount:-amount, amount:-amount, amount:-amount]


def band_powers(start_field, margin, count, diagonal_ext, inside):
    fields = [start_field]
    margins = [margin]
    for degree in range(count):
        current = fields[-1]
        out_margin = margins[-1] - 1
        trim = S - out_margin
        images = apply_operator(current, crop_margin(diagonal_ext, trim)) * crop_margin(
            inside, trim
        )
        previous = crop_margin(fields[-2], 2) if degree else None
        fields.append(chebyshev_next(images, crop_margin(current, 1), previous))
        margins.append(out_margin)
    return [crop_margin(one_field, edge_width) for one_field, edge_width in zip(fields, margins)]


def body(right_side, diagonal):
    block_z, block_y, block_x = diagonal.shape
    solution = jnp.zeros(right_side.shape, jnp.float32)
    residual = right_side
    direction = right_side
    diagonal_ext = extended_2(diagonal, (("gz", 0), ("gy", 1), ("gx", 2)), S, False)
    ext_shape = diagonal_ext.shape
    z_index = lax.broadcasted_iota(jnp.int32, ext_shape, 0) + lax.axis_index("gz") * block_z - S
    y_index = lax.broadcasted_iota(jnp.int32, ext_shape, 1) + lax.axis_index("gy") * block_y - S
    x_index = lax.broadcasted_iota(jnp.int32, ext_shape, 2) + lax.axis_index("gx") * block_x - S
    inside = (
        (z_index >= 0)
        & (z_index < block_z * lax.axis_size("gz"))
        & (y_index >= 0)
        & (y_index < block_y * lax.axis_size("gy"))
        & (x_index >= 0)
        & (x_index < block_x * lax.axis_size("gx"))
    ).astype(jnp.float32)
    for outer_step in range(OUTER):
        extended = extended_2(
            jnp.stack([direction, residual]), (("gz", 1), ("gy", 2), ("gx", 3)), S, False
        )
        p_fields = band_powers(extended[0], S, S, diagonal_ext, inside)
        r_fields = band_powers(crop_margin(extended[1], 1), S - 1, S - 1, diagonal_ext, inside)
        basis_set = jnp.stack(p_fields + r_fields)
        flattened = basis_set.reshape(basis_set.shape[0], -1)
        local_gram = jnp.dot(flattened, flattened.T, precision=lax.Precision.HIGHEST)
        gram_matrix = lax.psum(local_gram, ("gz", "gy", "gx"))
        sol_coeff, res_coeff, dir_coeff = coefficients(gram_matrix)
        solution = solution + combine(sol_coeff, basis_set)
        residual = combine(res_coeff, basis_set)
        direction = combine(dir_coeff, basis_set)
    return (solution, residual)


def solution(mesh):
    placed = (P("gz", "gy", "gx"), P("gz", "gy", "gx"))
    return jax.shard_map(
        body,
        mesh=mesh,
        in_specs=placed,
        out_specs=(P("gz", "gy", "gx"), P("gz", "gy", "gx")),
        check_vma=False,
    )
```

profile of v0, /device:TPU:0, one launch (start us, length us, event | category | flops | bytes accessed | tf_op | source)
XLA Modules:
  0.0 653.1 jit_solution(13936170096167725137)
XLA Ops:
  2.9 5.6 collective-permute-start.6
  9.5 3.9 collective-permute-start
  16.0 3.4 collective-permute-start.8
  20.8 4.6 collective-permute-start.2
  36.9 3.7 collective-permute-start.4
  53.6 3.4 fusion.125
  68.1 40.7 %psum.35 = f32[13,13]{1,0:T(8,128)S(1)} all-reduce(f32[13,13]{1,0:T(8,128)S(1)} %convolution_bitcast_fusion), channel_id=1, replica_groups=mesh['gz'=4,'gy'=4,'gx'=2] {'gz','gy','gx'}, use_global_device_ids=true, to_apply=%region_0.0 | all-reduce | flops 169 | bytes 1352 | tf_op jit(solution)/shard_map/psum | solution.py:158
  140.9 4.3 collective-permute-done.13
  145.3 4.2 collective-permute-start.14
  152.3 4.7 collective-permute-done.15
  171.6 3.1 fusion.121
  174.8 3.0 fusion.217
  193.9 40.9 %psum.36 = f32[13,13]{1,0:T(8,128)S(1)} all-reduce(f32[13,13]{1,0:T(8,128)S(1)} %fusion.33), channel_id=1, replica_groups=mesh['gz'=4,'gy'=4,'gx'=2] {'gz','gy','gx'}, use_global_device_ids=true, to_apply=%region_1.0 | all-reduce | flops 169 | bytes 1352 | tf_op jit(solution)/shard_map/psum | solution.py:158
  267.9 4.3 collective-permute-done.19
  272.3 4.2 collective-permute-start.20
  279.3 4.4 collective-permute-done.21
  299.9 3.1 fusion.117
  303.1 3.0 fusion.209
  323.1 41.6 %psum.37 = f32[13,13]{1,0:T(8,128)S(1)} all-reduce(f32[13,13]{1,0:T(8,128)S(1)} %fusion.36), channel_id=1, replica_groups=mesh['gz'=4,'gy'=4,'gx'=2] {'gz','gy','gx'}, use_global_device_ids=true, to_apply=%region_2.0 | all-reduce | flops 169 | bytes 1352 | tf_op jit(solution)/shard_map/psum | solution.py:158
  400.2 4.3 collective-permute-done.25
  404.6 4.2 collective-permute-start.26
  411.6 4.4 collective-permute-done.27
  422.2 4.5 collective-permute-start.28
  433.3 3.1 fusion.113
  436.5 3.0 fusion.201
  455.7 40.0 %psum.38 = f32[13,13]{1,0:T(8,128)S(1)} all-reduce(f32[13,13]{1,0:T(8,128)S(1)} %fusion.39), channel_id=1, replica_groups=mesh['gz'=4,'gy'=4,'gx'=2] {'gz','gy','gx'}, use_global_device_ids=true, to_apply=%region_3.0 | all-reduce | flops 169 | bytes 1352 | tf_op jit(solution)/shard_map/psum | solution.py:158
  529.3 4.0 collective-permute-done.31
  533.4 4.2 collective-permute-start.32
  540.4 4.7 collective-permute-done.33
  550.7 4.4 collective-permute-start.34
  561.4 3.1 fusion.109
  583.6 40.3 %psum.39 = f32[13,13]{1,0:T(8,128)S(1)} all-reduce(f32[13,13]{1,0:T(8,128)S(1)} %fusion.30), channel_id=1, replica_groups=mesh['gz'=4,'gy'=4,'gx'=2] {'gz','gy','gx'}, use_global_device_ids=true, to_apply=%region_4.0 | all-reduce | flops 169 | bytes 1352 | tf_op jit(solution)/shard_map/psum | solution.py:158
  (519 shorter events, 259.9 us)
Async XLA Ops:
  1.6 14.3 %collective-permute-start.7 = (f32[6,16,128]{2,1,0:T(8,128)S(1)}, f32[6,16,128]{2,1,0:T(8,128)S(1)}, u32[]{:S(2)}, u32[]{:S(2)}) collective-permute-start(f32[6,16,128]{2,1,0:T(8,128)S(1)} %get-tuple-element.44), channel_id=1, source_target_pairs={{8,0},{16,8},{24,16},{9,1},{17,9},{25,17},{10,2},{18,10},{26,18},{... | collective-permute-start | bytes 147464 | tf_op jit(solution)/shard_map/ppermute | solution.py:25
  2.9 13.0 %collective-permute-start.6 = (f32[6,16,128]{2,1,0:T(8,128)S(1)}, f32[6,16,128]{2,1,0:T(8,128)S(1)}, u32[]{:S(2)}, u32[]{:S(2)}) collective-permute-start(f32[6,16,128]{2,1,0:T(8,128)S(1)} %get-tuple-element.45), channel_id=1, source_target_pairs={{0,8},{8,16},{16,24},{1,9},{9,17},{17,25},{2,10},{10,18},{18,26},{... | collective-permute-start | bytes 147464 | tf_op jit(solution)/shard_map/ppermute | solution.py:22
  9.5 11.2 %collective-permute-start = (f32[2,6,16,128]{3,2,1,0:T(8,128)S(1)}, f32[2,6,16,128]{3,2,1,0:T(8,128)S(1)}, u32[]{:S(2)}, u32[]{:S(2)}) collective-permute-start(f32[2,6,16,128]{3,2,1,0:T(8,128)S(1)} %get-tuple-element.46), channel_id=1, source_target_pairs={{0,8},{8,16},{16,24},{1,9},{9,17},{17,25},{2,10},{10,18},{18,26},{... | collective-permute-start | bytes 294920 | tf_op jit(solution)/shard_map/ppermute | solution.py:22
  13.4 7.3 %collective-permute-start.1 = (f32[2,6,16,128]{3,2,1,0:T(8,128)S(1)}, f32[2,6,16,128]{3,2,1,0:T(8,128)S(1)}, u32[]{:S(2)}, u32[]{:S(2)}) collective-permute-start(f32[2,6,16,128]{3,2,1,0:T(8,128)S(1)} %get-tuple-element.47), channel_id=1, source_target_pairs={{8,0},{16,8},{24,16},{9,1},{17,9},{25,17},{10,2},{18,10},{26,18},{... | collective-permute-start | bytes 294920 | tf_op jit(solution)/shard_map/ppermute | solution.py:25
  16.0 10.7 %collective-permute-start.8 = (f32[20,6,128]{2,1,0:T(8,128)S(1)}, f32[20,6,128]{2,1,0:T(8,128)S(1)}, u32[]{:S(2)}, u32[]{:S(2)}) collective-permute-start(f32[20,6,128]{2,1,0:T(8,128)S(1)} %get-tuple-element.34), channel_id=1, source_target_pairs={{0,2},{2,4},{4,6},{1,3},{3,5},{5,7},{8,10},{10,12},{12,14},{9,11},... | collective-permute-start | bytes 184328 | tf_op jit(solution)/shard_map/ppermute | solution.py:22
  19.4 7.3 %collective-permute-start.9 = (f32[20,6,128]{2,1,0:T(8,128)S(1)}, f32[20,6,128]{2,1,0:T(8,128)S(1)}, u32[]{:S(2)}, u32[]{:S(2)}) collective-permute-start(f32[20,6,128]{2,1,0:T(8,128)S(1)} %get-tuple-element.35), channel_id=1, source_target_pairs={{2,0},{4,2},{6,4},{3,1},{5,3},{7,5},{10,8},{12,10},{14,12},{11,9},... | collective-permute-start | bytes 184328 | tf_op jit(solution)/shard_map/ppermute | solution.py:25
  20.8 10.1 %collective-permute-start.2 = (f32[2,20,6,128]{3,2,1,0:T(8,128)S(1)}, f32[2,20,6,128]{3,2,1,0:T(8,128)S(1)}, u32[]{:S(2)}, u32[]{:S(2)}) collective-permute-start(f32[2,20,6,128]{3,2,1,0:T(8,128)S(1)} %get-tuple-element.32), channel_id=1, source_target_pairs={{0,2},{2,4},{4,6},{1,3},{3,5},{5,7},{8,10},{10,12},{12,14},{9,11},... | collective-permute-start | bytes 368648 | tf_op jit(solution)/shard_map/ppermute | solution.py:22
  25.3 8.6 %collective-permute-start.3 = (f32[2,20,6,128]{3,2,1,0:T(8,128)S(1)}, f32[2,20,6,128]{3,2,1,0:T(8,128)S(1)}, u32[]{:S(2)}, u32[]{:S(2)}) collective-permute-start(f32[2,20,6,128]{3,2,1,0:T(8,128)S(1)} %get-tuple-element.33), channel_id=1, source_target_pairs={{2,0},{4,2},{6,4},{3,1},{5,3},{7,5},{10,8},{12,10},{14,12},{11,9},... | collective-permute-start | bytes 368648 | tf_op jit(solution)/shard_map/ppermute | solution.py:25
  27.6 13.0 %collective-permute-start.10 = (f32[20,28,6]{2,1,0:T(8,128)}, f32[20,28,6]{2,1,0:T(8,128)}, u32[]{:S(2)}, u32[]{:S(2)}) collective-permute-start(f32[20,28,6]{2,1,0:T(8,128)} %get-tuple-element.30), channel_id=1, source_target_pairs={{0,1},{2,3},{4,5},{6,7},{8,9},{10,11},{12,13},{14,15},{16,17},{18,... | collective-permute-start | bytes 40328 | tf_op jit(solution)/shard_map/ppermute | solution.py:22
  29.6 11.0 %collective-permute-start.11 = (f32[20,28,6]{2,1,0:T(8,128)S(1)}, f32[20,28,6]{2,1,0:T(8,128)}, u32[]{:S(2)}, u32[]{:S(2)}) collective-permute-start(f32[20,28,6]{2,1,0:T(8,128)S(1)} %get-tuple-element.31), channel_id=1, source_target_pairs={{1,0},{3,2},{5,4},{7,6},{9,8},{11,10},{13,12},{15,14},{17,16},{19,... | collective-permute-start | bytes 40328 | tf_op jit(solution)/shard_map/ppermute | solution.py:25
  35.6 7.8 %collective-permute-start.5 = (f32[2,20,28,6]{2,0,3,1:T(2,128)S(1)}, f32[2,20,28,6]{2,0,3,1:T(2,128)S(1)}, u32[]{:S(2)}, u32[]{:S(2)}) collective-permute-start(f32[2,20,28,6]{2,0,3,1:T(2,128)S(1)} %copy.30), channel_id=1, source_target_pairs={{1,0},{3,2},{5,4},{7,6},{9,8},{11,10},{13,12},{15,14},{17,16},{19,... | collective-permute-start | bytes 80648 | tf_op jit(solution)/shard_map/ppermute | solution.py:25
  36.9 5.2 collective-permute-start.4
  138.7 6.5 collective-permute-start.13
  145.3 7.0 %collective-permute-start.14 = (f32[2,20,6,128]{3,2,1,0:T(8,128)S(1)}, f32[2,20,6,128]{3,2,1,0:T(8,128)S(1)}, u32[]{:S(2)}, u32[]{:S(2)}) collective-permute-start(f32[2,20,6,128]{3,2,1,0:T(8,128)S(1)} %get-tuple-element.28), channel_id=1, source_target_pairs={{0,2},{2,4},{4,6},{1,3},{3,5},{5,7},{8,10},{10,12},{12,14},{9,11},... | collective-permute-start | bytes 368648 | tf_op jit(solution)/shard_map/ppermute | solution.py:22
  149.5 7.5 %collective-permute-start.15 = (f32[2,20,6,128]{3,2,1,0:T(8,128)S(1)}, f32[2,20,6,128]{3,2,1,0:T(8,128)S(1)}, u32[]{:S(2)}, u32[]{:S(2)}) collective-permute-start(f32[2,20,6,128]{3,2,1,0:T(8,128)S(1)} %get-tuple-element.29), channel_id=1, source_target_pairs={{2,0},{4,2},{6,4},{3,1},{5,3},{7,5},{10,8},{12,10},{14,12},{11,9},... | collective-permute-start | bytes 368648 | tf_op jit(solution)/shard_map/ppermute | solution.py:25
  160.9 4.4 collective-permute-start.16
  265.7 6.5 collective-permute-start.19
  272.3 7.0 %collective-permute-start.20 = (f32[2,20,6,128]{3,2,1,0:T(8,128)S(1)}, f32[2,20,6,128]{3,2,1,0:T(8,128)S(1)}, u32[]{:S(2)}, u32[]{:S(2)}) collective-permute-start(f32[2,20,6,128]{3,2,1,0:T(8,128)S(1)} %get-tuple-element.26), channel_id=1, source_target_pairs={{0,2},{2,4},{4,6},{1,3},{3,5},{5,7},{8,10},{10,12},{12,14},{9,11},... | collective-permute-start | bytes 368648 | tf_op jit(solution)/shard_map/ppermute | solution.py:22
  276.5 7.2 %collective-permute-start.21 = (f32[2,20,6,128]{3,2,1,0:T(8,128)S(1)}, f32[2,20,6,128]{3,2,1,0:T(8,128)S(1)}, u32[]{:S(2)}, u32[]{:S(2)}) collective-permute-start(f32[2,20,6,128]{3,2,1,0:T(8,128)S(1)} %get-tuple-element.27), channel_id=1, source_target_pairs={{2,0},{4,2},{6,4},{3,1},{5,3},{7,5},{10,8},{12,10},{14,12},{11,9},... | collective-permute-start | bytes 368648 | tf_op jit(solution)/shard_map/ppermute | solution.py:25
  287.9 5.5 collective-permute-start.22
  395.9 4.3 collective-permute-start.24
  398.0 6.5 collective-permute-start.25
  404.6 7.0 %collective-permute-start.26 = (f32[2,20,6,128]{3,2,1,0:T(8,128)S(1)}, f32[2,20,6,128]{3,2,1,0:T(8,128)S(1)}, u32[]{:S(2)}, u32[]{:S(2)}) collective-permute-start(f32[2,20,6,128]{3,2,1,0:T(8,128)S(1)} %get-tuple-element.24), channel_id=1, source_target_pairs={{0,2},{2,4},{4,6},{1,3},{3,5},{5,7},{8,10},{10,12},{12,14},{9,11},... | collective-permute-start | bytes 368648 | tf_op jit(solution)/shard_map/ppermute | solution.py:22
  408.8 7.2 %collective-permute-start.27 = (f32[2,20,6,128]{3,2,1,0:T(8,128)S(1)}, f32[2,20,6,128]{3,2,1,0:T(8,128)S(1)}, u32[]{:S(2)}, u32[]{:S(2)}) collective-permute-start(f32[2,20,6,128]{3,2,1,0:T(8,128)S(1)} %get-tuple-element.25), channel_id=1, source_target_pairs={{2,0},{4,2},{6,4},{3,1},{5,3},{7,5},{10,8},{12,10},{14,12},{11,9},... | collective-permute-start | bytes 368648 | tf_op jit(solution)/shard_map/ppermute | solution.py:25
  420.9 9.0 %collective-permute-start.29 = (f32[2,20,28,6]{2,0,3,1:T(2,128)S(1)}, f32[2,20,28,6]{2,0,3,1:T(2,128)}, u32[]{:S(2)}, u32[]{:S(2)}) collective-permute-start(f32[2,20,28,6]{2,0,3,1:T(2,128)S(1)} %copy.58), channel_id=1, source_target_pairs={{1,0},{3,2},{5,4},{7,6},{9,8},{11,10},{13,12},{15,14},{17,16},{19,... | collective-permute-start | bytes 80648 | tf_op jit(solution)/shard_map/ppermute | solution.py:25
  422.2 6.4 collective-permute-start.28
  524.6 4.8 collective-permute-start.30
  526.8 6.5 collective-permute-start.31
  533.4 7.0 %collective-permute-start.32 = (f32[2,20,6,128]{3,2,1,0:T(8,128)S(1)}, f32[2,20,6,128]{3,2,1,0:T(8,128)S(1)}, u32[]{:S(2)}, u32[]{:S(2)}) collective-permute-start(f32[2,20,6,128]{3,2,1,0:T(8,128)S(1)} %get-tuple-element.22), channel_id=1, source_target_pairs={{0,2},{2,4},{4,6},{1,3},{3,5},{5,7},{8,10},{10,12},{12,14},{9,11},... | collective-permute-start | bytes 368648 | tf_op jit(solution)/shard_map/ppermute | solution.py:22
  537.6 7.5 %collective-permute-start.33 = (f32[2,20,6,128]{3,2,1,0:T(8,128)S(1)}, f32[2,20,6,128]{3,2,1,0:T(8,128)S(1)}, u32[]{:S(2)}, u32[]{:S(2)}) collective-permute-start(f32[2,20,6,128]{3,2,1,0:T(8,128)S(1)} %get-tuple-element.23), channel_id=1, source_target_pairs={{2,0},{4,2},{6,4},{3,1},{5,3},{7,5},{10,8},{12,10},{14,12},{11,9},... | collective-permute-start | bytes 368648 | tf_op jit(solution)/shard_map/ppermute | solution.py:25
  549.4 8.8 %collective-permute-start.35 = (f32[2,20,28,6]{2,0,3,1:T(2,128)S(1)}, f32[2,20,28,6]{2,0,3,1:T(2,128)}, u32[]{:S(2)}, u32[]{:S(2)}) collective-permute-start(f32[2,20,28,6]{2,0,3,1:T(2,128)S(1)} %copy.64), channel_id=1, source_target_pairs={{1,0},{3,2},{5,4},{7,6},{9,8},{11,10},{13,12},{15,14},{17,16},{19,... | collective-permute-start | bytes 80648 | tf_op jit(solution)/shard_map/ppermute | solution.py:25
  550.7 6.3 collective-permute-start.34
  (69 other events, 1713.1 us)
where the time goes:
time: 666 us; the launch traced here: 653 us
  blocking collectives  203 us (30%)
  other arithmetic  111 us (17%)
  starting transfers between devices  84.9 us (13%)
  between operations  82.8 us (12%)
  matrix products  79.3 us (12%)
  waiting for transfers between devices  46.6 us (7%)
  local copies, waits for them, and re-layouts  45.6 us (7%)
    psum x5, blocking collectives, body(): gram_matrix = lax.psum(local_gram, ('gz', 'gy', 'gx'))  203 us
    sub x37, other arithmetic, chebyshev_next(): return 2.0 * scaled - previous  63.6 us
    ppermute x18, starting transfers between devices, extended_2(): lax.ppermute(lax.slice_in_dim(block, block.shape[dim] - width, None, axis...  61.3 us
    ppermute x18, waiting for transfers between devices, extended_2(): lax.ppermute(lax.slice_in_dim(block, 0, width, axis=dim), axis, backward)  39 us
    div x10, other arithmetic, chebyshev_next(): scaled = (images - center_shift * current) / half_width  31 us
    ppermute x18, starting transfers between devices, extended_2(): lax.ppermute(lax.slice_in_dim(block, 0, width, axis=dim), axis, backward)  23.5 us
    dot_general x30, matrix products, coefficients(): jnp.dot(gram_matrix, moved, precision=lax.Precision.HIGHEST)  22.7 us
    dot_general x30, matrix products, coefficients(): jnp.dot(gram_matrix, res_coeff, precision=lax.Precision.HIGHEST)  22.3 us
  transfers between devices with their start and end apart: 36, of which 17 were waited for; matrix products, arithmetic and copies ran while one was open for 3% of the time, Pallas kernels for 0%

commit v1 on v0

v1 whole, which is shorter than its diff:
```python
import jax
import jax.numpy as jnp
import numpy as np
from jax import lax
from jax.experimental import pallas as pl
from jax.experimental.pallas import tpu as pltpu
from jax.sharding import PartitionSpec as P

S = 6
OUTER = 5
COLS = 2 * S + 1
SHIFT = 19.0
HALF = 19.0
LANES = 128
ROWS = 8
MESH = pl.DeviceIdType.MESH


def basis_change():
    matrix = np.zeros((COLS, COLS), np.float32)
    for offset, length in ((0, S), (S + 1, S - 1)):
        for degree in range(length):
            matrix[offset + degree, offset + degree] = SHIFT
            if degree == 0:
                matrix[offset + 1, offset] = HALF
            else:
                matrix[offset + degree + 1, offset + degree] = 0.5 * HALF
                matrix[offset + degree - 1, offset + degree] = 0.5 * HALF
    return matrix


def table(index, values):
    out = jnp.zeros(index.shape, jnp.float32)
    for position, value in enumerate(values):
        if value:
            out = jnp.where(index == position, jnp.float32(value), out)
    return out


def kernel(nz, ny, nx, rhs_ref, diag_ref, sol_out, res_out,
           fields, p_chain, r_chain, scale2, weight, total, pairs, g_send, g_recv, final,
           z_send, z_recv, y_send, y_recv, g_ssem, g_rsem, swap_send, swap_recv, own_sem):
    bz, by, bx = rhs_ref.shape
    hy = by // 2
    ze, halves, ya = fields.shape[1:4]
    first = (ya - hy) // 2
    low_rows, high_rows = slice(first - ROWS, first), slice(first + hy, first + hy + ROWS)
    iz, iy, ix = lax.axis_index("gz"), lax.axis_index("gy"), lax.axis_index("gx")
    other = 1 - ix
    yy = iy * 2 + ix
    count = nz * ny * nx
    me = (iz * ny + iy) * nx + ix
    has_z = (iz > 0, iz < nz - 1)
    has_y = (yy > 0, yy < 2 * ny - 1)
    z_dev = tuple((iz + s, iy, ix) for s in (-1, 1))
    y_dev = tuple((iz, (yy + s) // 2, other) for s in (-1, 1))
    mid_z, mid_y = slice(S, S + bz), slice(first, first + hy)

    def row_tile(index):
        return pl.ds(pl.multiple_of(index * hy, hy), hy)

    swaps, owns = [], []
    for k, ref in enumerate((rhs_ref, diag_ref)):
        spot = fields.at[1 + k, mid_z, ix, mid_y, :]
        swap = pltpu.make_async_remote_copy(
            src_ref=ref.at[:, row_tile(other), :], dst_ref=spot,
            send_sem=swap_send.at[k], recv_sem=swap_recv.at[k],
            device_id=(iz, iy, other), device_id_type=MESH)
        swap.start()
        own = pltpu.make_async_copy(ref.at[:, row_tile(ix), :], spot, own_sem.at[k])
        own.start()
        swaps.append(swap)
        owns.append(own)

    for side in range(2):
        planes = slice(0, S) if side == 0 else slice(S + bz, ze)
        rows = (low_rows, high_rows)[side]

        @pl.when(jnp.logical_not(has_z[side]))
        def _():
            for k in (0, 1, 2):
                fields[k, planes] = jnp.zeros((S, halves, ya, bx), jnp.float32)

        @pl.when(jnp.logical_not(has_y[side]))
        def _():
            for k in (0, 1, 2):
                fields[k, :, :, rows, :] = jnp.zeros((ze, halves, ROWS, bx), jnp.float32)

    w_unit = 2.0 / HALF
    w_low = jnp.where(has_y[0], jnp.float32(w_unit), 0.0)
    w_high = jnp.where(has_y[1], jnp.float32(w_unit), 0.0)
    z_low = jnp.where(has_z[0], jnp.float32(1.0), 0.0)
    z_high = jnp.where(has_z[1], jnp.float32(1.0), 0.0)
    for plane in range(ze):
        factor = z_low if plane < S else (z_high if plane >= S + bz else jnp.float32(1.0))
        for tile, w in enumerate((w_low, jnp.float32(w_unit), w_high)):
            weight[plane, tile] = jnp.broadcast_to(w * factor, (ROWS, bx))
    total[...] = jnp.zeros(total.shape, jnp.float32)
    pairs[...] = jnp.zeros(pairs.shape, jnp.float32)

    for copy in owns + swaps:
        copy.wait()

    def z_copy(lo, side):
        src = slice(S, 2 * S) if side == 0 else slice(bz, bz + S)
        dst = slice(S + bz, ze) if side == 0 else slice(0, S)
        return pltpu.make_async_remote_copy(
            src_ref=fields.at[lo:lo + 2, src, :, mid_y, :], dst_ref=fields.at[lo:lo + 2, dst, :, mid_y, :],
            send_sem=z_send.at[side], recv_sem=z_recv.at[1 - side],
            device_id=z_dev[side], device_id_type=MESH)

    def y_copy(lo, side, part):
        planes = (mid_z, slice(0, S), slice(S + bz, ze))[part]
        dst = (high_rows, low_rows)[side]
        return pltpu.make_async_remote_copy(
            src_ref=fields.at[lo:lo + 2, planes, :, mid_y, :], dst_ref=fields.at[lo:lo + 2, planes, :, dst, :],
            send_sem=y_send.at[side, part], recv_sem=y_recv.at[1 - side, part],
            device_id=y_dev[side], device_id_type=MESH)

    def exchange(lo):
        for side in range(2):
            @pl.when(has_z[side])
            def _():
                z_copy(lo, side).start()
        for side in range(2):
            @pl.when(has_y[side])
            def _():
                y_copy(lo, side, 0).start()
        for z_side in range(2):
            @pl.when(has_z[z_side])
            def _():
                z_copy(lo, 1 - z_side).wait_recv()
                for side in range(2):
                    @pl.when(has_y[side])
                    def _():
                        y_copy(lo, side, 1 + z_side).start()
        for side in range(2):
            @pl.when(has_z[side])
            def _():
                z_copy(lo, side).wait_send()

            @pl.when(has_y[side])
            def _():
                y_copy(lo, side, 0).wait_send()
                y_copy(lo, 1 - side, 0).wait_recv()
                for z_side in range(2):
                    @pl.when(has_z[z_side])
                    def _():
                        y_copy(lo, side, 1 + z_side).wait_send()
                        y_copy(lo, 1 - side, 1 + z_side).wait_recv()

    exchange(1)
    all_rows = slice(first - ROWS, first + hy + ROWS)

    def prepare(plane, c):
        fields[0, plane] = fields[1, plane]
        scale2[plane] = (fields[2, plane, :, all_rows, :] + (27.0 - SHIFT)) * (2.0 / HALF)
        return c
    lax.fori_loop(0, ze, prepare, 0)

    tiles = (hy + 2 * ROWS) // ROWS
    lane_id = lax.broadcasted_iota(jnp.int32, (ROWS, bx), 1)
    first_lane, last_lane = lane_id == 0, lane_id == bx - 1

    def row_sums(ref, z, tile):
        at = first - ROWS + tile * ROWS
        return [ref[z, h, at - 1:at - 1 + ROWS, :] + ref[z, h, at:at + ROWS, :] + ref[z, h, at + 1:at + 1 + ROWS, :]
                for h in range(halves)]

    def lane_sums(parts):
        left = [pltpu.roll(v, 1, 1) for v in parts]
        right = [pltpu.roll(v, bx - 1, 1) for v in parts]
        out = []
        for h in range(halves):
            before = left[h - 1] if h else 0.0
            after = right[h + 1] if h < halves - 1 else 0.0
            out.append(parts[h] + jnp.where(first_lane, before, left[h]) + jnp.where(last_lane, after, right[h]))
        return out

    p_at = [fields.at[1]] + [p_chain.at[k] for k in range(S)]
    r_at = [fields.at[0]] + [r_chain.at[k] for k in range(S - 1)]

    def degree_sweep(chains, degree, start, stop, chosen):
        jobs = [(chain, tile) for chain in chains for tile in chosen]

        def step(z, carry):
            out = []
            for (chain, tile), (before, here) in zip(jobs, carry):
                after = row_sums(chain[degree], z + 1, tile)
                box = lane_sums([a + b + c for a, b, c in zip(before, here, after)])
                at = first - ROWS + tile * ROWS
                for h in range(halves):
                    value = (scale2[z, h, tile * ROWS:(tile + 1) * ROWS, :] * chain[degree][z, h, at:at + ROWS, :]
                             - weight[z, tile] * box[h])
                    if degree == 0:
                        value = 0.5 * value
                    else:
                        value = value - chain[degree - 1][z, h, at:at + ROWS, :]
                    chain[degree + 1][z, h, at:at + ROWS, :] = value
                out.append((here, after))
            return tuple(out)
        init = tuple((row_sums(c[degree], start - 1, k), row_sums(c[degree], start, k)) for c, k in jobs)
        for z in range(start, stop):
            init = step(z, init)

    gl = lax.broadcasted_iota(jnp.int32, (2 * ROWS, LANES), 1)
    gr = lax.broadcasted_iota(jnp.int32, (2 * ROWS, LANES), 0)
    change = basis_change()
    diag_b = [change[i, i] for i in range(COLS)]
    low_b = [change[i, i - 1] if i else 0.0 for i in range(COLS)]
    up_b = [change[i, i + 1] if i < COLS - 1 else 0.0 for i in range(COLS)]
    b_row = [table(gl, v) for v in (diag_b, low_b, up_b)]
    b_col = [table(gr, v) for v in (diag_b, low_b, up_b)]

    def apply_b(col, row):
        q_row = b_row[0] * row + b_row[1] * pltpu.roll(row, 1, 1) + b_row[2] * pltpu.roll(row, LANES - 1, 1)
        q_col = b_col[0] * col + b_col[1] * pltpu.roll(col, 1, 0) + b_col[2] * pltpu.roll(col, 2 * ROWS - 1, 0)
        return q_col, q_row

    def outer(t, carry):
        for degree in range(S):
            if degree < S - 1:
                degree_sweep((p_at,), degree, degree + 1, ze - degree - 1, range(tiles))
                r_tiles = range(tiles) if degree < S - 2 else (1,)
                degree_sweep((r_at,), degree, degree + 2, ze - degree - 2, r_tiles)
            else:
                degree_sweep((p_at,), degree, degree + 1, ze - degree - 1, (1,))
        basis = p_at + r_at

        for lo_i, hi_i, lo_j in ((0, S + 1, 0), (0, S + 1, S + 1), (S + 1, COLS, S + 1)):
            hi_j = S + 1 if lo_j == 0 else COLS
            sums = {}
            for z in range(S, S + bz):
                for h in range(halves):
                    va = [basis[i][z, h, mid_y, :] for i in range(lo_i, hi_i)]
                    vb = va if lo_i == lo_j else [basis[j][z, h, mid_y, :] for j in range(lo_j, hi_j)]
                    for i in range(lo_i, hi_i):
                        for j in range(max(i, lo_j), hi_j):
                            term = va[i - lo_i] * vb[j - lo_j]
                            sums[i, j] = sums[i, j] + term if (i, j) in sums else term
            for (i, j), value in sums.items():
                line = jnp.sum(value, axis=0, keepdims=True)
                pairs[i * 16 + j:i * 16 + j + 1, :] = line
                if i != j:
                    pairs[j * 16 + i:j * 16 + i + 1, :] = line
        for half in range(2):
            turned = pairs[half * LANES:(half + 1) * LANES, :].T
            g_send[half:half + 1, :] = jnp.sum(turned, axis=0, keepdims=True)

        slot = t % 2
        own = pltpu.make_async_copy(g_send, g_recv.at[slot, me], g_rsem.at[slot])
        own.start()

        def send(d, c):
            peer = (me + d) % count
            pltpu.make_async_remote_copy(
                src_ref=g_send, dst_ref=g_recv.at[slot, me],
                send_sem=g_ssem, recv_sem=g_rsem.at[slot],
                device_id=(peer // (ny * nx), (peer // nx) % ny, peer % nx), device_id_type=MESH).start()
            return c
        lax.fori_loop(1, count, send, 0)
        everything = g_recv.at[slot]
        pltpu.make_async_copy(everything, everything, g_rsem.at[slot]).wait()
        most = g_recv.at[slot, 0:count - 1]
        pltpu.make_async_copy(most, most, g_ssem).wait()
        rows2 = jnp.sum(g_recv[slot], axis=0)
        gram = jnp.zeros((2 * ROWS, LANES), jnp.float32)
        for half in range(2):
            line = jnp.broadcast_to(rows2[half:half + 1, :], (2 * ROWS, LANES))
            for k in range(8):
                i = half * 8 + k
                if i < COLS:
                    moved = line if k == 0 else pltpu.roll(line, LANES - 16 * k, 1)
                    gram = jnp.where(gr == i, moved, gram)
        gram = jnp.where(gl < COLS, gram, 0.0)

        def quad(col, row):
            return jnp.sum(jnp.sum(gram * col * row, axis=0, keepdims=True), axis=1, keepdims=True)

        p_row, p_col = (gl == 0).astype(jnp.float32), (gr == 0).astype(jnp.float32)
        r_row, r_col = (gl == S + 1).astype(jnp.float32), (gr == S + 1).astype(jnp.float32)
        x_col = jnp.zeros((2 * ROWS, LANES), jnp.float32)
        norm = quad(r_col, r_row)
        for _ in range(S):
            q_col, q_row = apply_b(p_col, p_row)
            length = norm / quad(p_col, q_row)
            x_col = x_col + length * p_col
            r_col = r_col - length * q_col
            r_row = r_row - length * q_row
            fresh = quad(r_col, r_row)
            ratio = fresh / norm
            p_col = r_col + ratio * p_col
            p_row = r_row + ratio * p_row
            norm = fresh

        def weights(col):
            return [jnp.broadcast_to(col[i:i + 1, :], (hy, LANES)) for i in range(COLS)]

        xw, rw, pw = weights(x_col), weights(r_col), weights(p_col)
        for z in range(bz):
            for h in range(halves):
                vs = [b[S + z, h, mid_y, :] for b in basis]

                def mix(w):
                    out = w[0] * vs[0]
                    for a, b in zip(w[1:], vs[1:]):
                        out = out + a * b
                    return out
                total[0, z, h] = total[0, z, h] + mix(xw)
                fields[0, S + z, h, mid_y, :] = mix(rw)
                fields[1, S + z, h, mid_y, :] = mix(pw)

        @pl.when(t < OUTER - 1)
        def _():
            exchange(0)
        return carry

    lax.fori_loop(0, OUTER, outer, 0)

    total[1] = fields[0, mid_z, :, mid_y, :]
    back = pltpu.make_async_remote_copy(
        src_ref=total.at[:, :, other], dst_ref=final,
        send_sem=swap_send.at[0], recv_sem=swap_recv.at[0],
        device_id=(iz, iy, other), device_id_type=MESH)
    back.start()
    for k, out in enumerate((sol_out, res_out)):
        out[:, row_tile(ix), :] = total[k, :, ix]
    back.wait()
    for k, out in enumerate((sol_out, res_out)):
        out[:, row_tile(other), :] = final[k]


def solution(mesh):
    nz, ny, nx = mesh.shape["gz"], mesh.shape["gy"], mesh.shape["gx"]
    count = nz * ny * nx

    def body(right_side, diagonal):
        bz, by, bx = right_side.shape
        hy = by // 2
        assert nx == 2 and bz >= S and hy == ROWS and bx == LANES
        ze, ye = bz + 2 * S, hy + 4 * ROWS
        f32, dma = jnp.float32, pltpu.SemaphoreType.DMA
        return pl.pallas_call(
            lambda *refs: kernel(nz, ny, nx, *refs),
            out_shape=(jax.ShapeDtypeStruct(right_side.shape, f32),) * 2,
            in_specs=[pl.BlockSpec(memory_space=pltpu.VMEM)] * 2,
            out_specs=(pl.BlockSpec(memory_space=pltpu.VMEM),) * 2,
            scratch_shapes=[
                pltpu.VMEM((3, ze, nx, ye, bx), f32),
                pltpu.VMEM((S, ze, nx, ye, bx), f32),
                pltpu.VMEM((S - 1, ze, nx, ye, bx), f32),
                pltpu.VMEM((ze, nx, hy + 2 * ROWS, bx), f32),
                pltpu.VMEM((ze, 3, ROWS, bx), f32),
                pltpu.VMEM((2, bz, nx, hy, bx), f32),
                pltpu.VMEM((2 * LANES, LANES), f32),
                pltpu.VMEM((2, LANES), f32),
                pltpu.VMEM((2, count, 2, LANES), f32),
                pltpu.VMEM((2, bz, hy, bx), f32),
                dma((2,)), dma((2,)), dma((2, 3)), dma((2, 3)),
                dma, dma((2,)), dma((2,)), dma((2,)), dma((2,)),
            ],
            compiler_params=pltpu.CompilerParams(has_side_effects=True),
        )(right_side, diagonal)

    spec = P("gz", "gy", "gx")
    return jax.shard_map(body, mesh=mesh, in_specs=(spec, spec), out_specs=(spec, spec), check_vma=False)
```

time: 666 us -> 103 us (0.15); the launches traced: 653 us -> 103 us
  blocking collectives: 203 us -> 0 us
  other arithmetic: 111 us -> 0 us
  Pallas kernels: 0 us -> 99.8 us
  starting transfers between devices: 84.9 us -> 0 us
  between operations: 82.8 us -> 0.65 us
  matrix products: 79.3 us -> 0 us
  waiting for transfers between devices: 46.6 us -> 0 us
  local copies, waits for them, and re-layouts: 45.6 us -> 2.14 us
    psum x5 -> x0, blocking collectives: 203 us -> none  [body(): gram_matrix = lax.psum(local_gram, ('gz', 'gy', 'gx'))]
    pallas_call x0 -> x1, Pallas kernels: none -> 99.8 us  [body(): pl.pallas_call(lambda *refs: kernel(nz, ny, nx, *refs), out_shape=(jax.Sh...]
    ppermute x36 -> x0, starting transfers between devices: 84.9 us -> none  [the longest x18 61.3 us: extended_2(): lax.ppermute(lax.slice_in_dim(block, block.shape[dim] - width, None, axis...]
    dot_general x109 -> x0, matrix products: 79.3 us -> none  [the longest x30 22.7 us: coefficients(): jnp.dot(gram_matrix, moved, precision=lax.Precision.HIGHEST)]
    sub x66 -> x0, other arithmetic: 63.7 us -> none  [the longest x37 63.6 us: chebyshev_next(): return 2.0 * scaled - previous]
    ppermute x36 -> x0, waiting for transfers between devices: 46.6 us -> none  [the longest x18 39 us: extended_2(): lax.ppermute(lax.slice_in_dim(block, 0, width, axis=dim), axis, backward)]
    div x10 -> x0, other arithmetic: 31 us -> none  [chebyshev_next(): scaled = (images - center_shift * current) / half_width]
    slice x34 -> x0, local copies, waits for them, and re-layouts: 21.7 us -> none  [the longest x17 14.6 us: extended_2(): lax.slice_in_dim(block, block.shape[dim] - width, None, axis=dim)]
  transfers between devices with their start and end apart: 36 -> 0, of which waited for: 17 -> 0; matrix products, arithmetic and copies ran while one was open for 3% -> 0% of each run, Pallas kernels for 0% -> 0%
where the time goes in v1:
time: 103 us
  Pallas kernels  99.8 us (97%)
  local copies, waits for them, and re-layouts  2.14 us (2%)
    pallas_call x1, Pallas kernels, body(): pl.pallas_call(lambda *refs: kernel(nz, ny, nx, *refs), out_shape=(jax.Sh...  99.8 us
    unnamed x4, local copies, waits for them, and re-layouts  2.14 us

profile of v1, /device:TPU:0, one launch (start us, length us, event | category | flops | bytes accessed | tf_op | source)
XLA Modules:
  0.0 102.6 jit_solution(10916551608181040052)
XLA Ops:
  0.6 99.8 %shard_map.41 = (f32[8,16,128]{2,1,0:T(8,128)}, f32[8,16,128]{2,1,0:T(8,128)}) custom-call(f32[8,16,128]{2,1,0:T(8,128)} %refs_0_.1, f32[8,16,128]{2,1,0:T(8,128)} %refs_1_.1), custom_call_target="tpu_custom_call" | custom-call | tf_op jit(solution)/shard_map/pallas_call | solution.py:343
  100.5 0.0 copy-start
  100.5 1.5 %copy.6 = f32[8,16,128]{2,1,0:T(8,128)} copy(f32[8,16,128]{2,1,0:T(8,128)} %get-tuple-element.4) | data formatting | bytes 131072
  102.0 0.0 copy-done
  102.0 0.6 copy.7
Async XLA Ops:
  100.5 1.5 %copy-start = (f32[8,16,128]{2,1,0:T(8,128)S(1)}, f32[8,16,128]{2,1,0:T(8,128)}, u32[]{:S(2)}) copy-start(f32[8,16,128]{2,1,0:T(8,128)} %get-tuple-element.5) | copy-start | bytes 196612

commit v2 on v1

--- a/solution.py
+++ b/solution.py
@@ -101,55 +101,65 @@
     for copy in owns + swaps:
         copy.wait()
 
-    def z_copy(lo, side):
-        src = slice(S, 2 * S) if side == 0 else slice(bz, bz + S)
-        dst = slice(S + bz, ze) if side == 0 else slice(0, S)
+    def z_copy(item, side):
+        field, depth, k = item
+        low_src, high_src = slice(S, S + depth), slice(S + bz - depth, S + bz)
+        low_dst, high_dst = slice(S - depth, S), slice(S + bz, S + bz + depth)
+        src, dst = ((low_src, high_dst), (high_src, low_dst))[side]
         return pltpu.make_async_remote_copy(
-            src_ref=fields.at[lo:lo + 2, src, :, mid_y, :], dst_ref=fields.at[lo:lo + 2, dst, :, mid_y, :],
-            send_sem=z_send.at[side], recv_sem=z_recv.at[1 - side],
+            src_ref=fields.at[field, src, :, mid_y, :], dst_ref=fields.at[field, dst, :, mid_y, :],
+            send_sem=z_send.at[k, side], recv_sem=z_recv.at[k, 1 - side],
             device_id=z_dev[side], device_id_type=MESH)
 
-    def y_copy(lo, side, part):
-        planes = (mid_z, slice(0, S), slice(S + bz, ze))[part]
-        dst = (high_rows, low_rows)[side]
+    def y_copy(item, side, part):
+        field, depth, k = item
+        planes = (mid_z, slice(S - depth, S), slice(S + bz, S + bz + depth))[part]
+        low_src, high_src = slice(first, first + depth), slice(first + hy - depth, first + hy)
+        low_dst, high_dst = slice(first - depth, first), slice(first + hy, first + hy + depth)
+        src, dst = ((low_src, high_dst), (high_src, low_dst))[side]
         return pltpu.make_async_remote_copy(
-            src_ref=fields.at[lo:lo + 2, planes, :, mid_y, :], dst_ref=fields.at[lo:lo + 2, planes, :, dst, :],
-            send_sem=y_send.at[side, part], recv_sem=y_recv.at[1 - side, part],
+            src_ref=fields.at[field, planes, :, src, :], dst_ref=fields.at[field, planes, :, dst, :],
+            send_sem=y_send.at[k, side, part], recv_sem=y_recv.at[k, 1 - side, part],
             device_id=y_dev[side], device_id_type=MESH)
 
-    def exchange(lo):
-        for side in range(2):
-            @pl.when(has_z[side])
-            def _():
-                z_copy(lo, side).start()
-        for side in range(2):
-            @pl.when(has_y[side])
-            def _():
-                y_copy(lo, side, 0).start()
-        for z_side in range(2):
-            @pl.when(has_z[z_side])
-            def _():
-                z_copy(lo, 1 - z_side).wait_recv()
-                for side in range(2):
-                    @pl.when(has_y[side])
-                    def _():
-                        y_copy(lo, side, 1 + z_side).start()
-        for side in range(2):
-            @pl.when(has_z[side])
-            def _():
-                z_copy(lo, side).wait_send()
-
-            @pl.when(has_y[side])
-            def _():
-                y_copy(lo, side, 0).wait_send()
-                y_copy(lo, 1 - side, 0).wait_recv()
-                for z_side in range(2):
-                    @pl.when(has_z[z_side])
-                    def _():
-                        y_copy(lo, side, 1 + z_side).wait_send()
-                        y_copy(lo, 1 - side, 1 + z_side).wait_recv()
-
-    exchange(1)
+    def exchange(shallow):
+        items = ((1, S, 0), (shallow, S - 1, 1))
+        for item in items:
+            for side in range(2):
+                @pl.when(has_z[side])
+                def _():
+                    z_copy(item, side).start()
+        for item in items:
+            for side in range(2):
+                @pl.when(has_y[side])
+                def _():
+                    y_copy(item, side, 0).start()
+        for item in items:
+            for z_side in range(2):
+                @pl.when(has_z[z_side])
+                def _():
+                    z_copy(item, 1 - z_side).wait_recv()
+                    for side in range(2):
+                        @pl.when(has_y[side])
+                        def _():
+                            y_copy(item, side, 1 + z_side).start()
+        for item in items:
+            for side in range(2):
+                @pl.when(has_z[side])
+                def _():
+                    z_copy(item, side).wait_send()
+
+                @pl.when(has_y[side])
+                def _():
+                    y_copy(item, side, 0).wait_send()
+                    y_copy(item, 1 - side, 0).wait_recv()
+                    for z_side in range(2):
+                        @pl.when(has_z[z_side])
+                        def _():
+                            y_copy(item, side, 1 + z_side).wait_send()
+                            y_copy(item, 1 - side, 1 + z_side).wait_recv()
+
+    exchange(2)
     all_rows = slice(first - ROWS, first + hy + ROWS)
 
     def prepare(plane, c):
@@ -212,6 +222,10 @@
     b_row = [table(gl, v) for v in (diag_b, low_b, up_b)]
     b_col = [table(gr, v) for v in (diag_b, low_b, up_b)]
 
+    b_down = [table(gl, v) for v in (
+        diag_b, [change[j + 1, j] if j < COLS - 1 else 0.0 for j in range(COLS)],
+        [change[j - 1, j] if j else 0.0 for j in range(COLS)])]
+
     def apply_b(col, row):
         q_row = b_row[0] * row + b_row[1] * pltpu.roll(row, 1, 1) + b_row[2] * pltpu.roll(row, LANES - 1, 1)
         q_col = b_col[0] * col + b_col[1] * pltpu.roll(col, 1, 0) + b_col[2] * pltpu.roll(col, 2 * ROWS - 1, 0)
@@ -248,17 +262,18 @@
             g_send[half:half + 1, :] = jnp.sum(turned, axis=0, keepdims=True)
 
         slot = t % 2
+        turn = jnp.where(iz * 2 < nz, -1, 1)
         own = pltpu.make_async_copy(g_send, g_recv.at[slot, me], g_rsem.at[slot])
         own.start()
 
-        def send(d, c):
-            peer = (me + d) % count
+        def send(k, c):
+            peer = (me + turn + turn * k + count) % count
             pltpu.make_async_remote_copy(
                 src_ref=g_send, dst_ref=g_recv.at[slot, me],
                 send_sem=g_ssem, recv_sem=g_rsem.at[slot],
                 device_id=(peer // (ny * nx), (peer // nx) % ny, peer % nx), device_id_type=MESH).start()
             return c
-        lax.fori_loop(1, count, send, 0)
+        lax.fori_loop(0, count - 1, send, 0, unroll=4)
         everything = g_recv.at[slot]
         pltpu.make_async_copy(everything, everything, g_rsem.at[slot]).wait()
         most = g_recv.at[slot, 0:count - 1]
@@ -274,20 +289,22 @@
                     gram = jnp.where(gr == i, moved, gram)
         gram = jnp.where(gl < COLS, gram, 0.0)
 
-        def quad(col, row):
-            return jnp.sum(jnp.sum(gram * col * row, axis=0, keepdims=True), axis=1, keepdims=True)
+        def quad(matrix, col, row):
+            return jnp.sum(jnp.sum(matrix * col * row, axis=0, keepdims=True), axis=1, keepdims=True)
+
+        moved_gram = (gram * b_down[0] + pltpu.roll(gram, LANES - 1, 1) * b_down[1] + pltpu.roll(gram, 1, 1) * b_down[2])
 
         p_row, p_col = (gl == 0).astype(jnp.float32), (gr == 0).astype(jnp.float32)
         r_row, r_col = (gl == S + 1).astype(jnp.float32), (gr == S + 1).astype(jnp.float32)
         x_col = jnp.zeros((2 * ROWS, LANES), jnp.float32)
-        norm = quad(r_col, r_row)
+        norm = quad(gram, r_col, r_row)
         for _ in range(S):
             q_col, q_row = apply_b(p_col, p_row)
-            length = norm / quad(p_col, q_row)
+            length = norm / quad(moved_gram, p_col, p_row)
             x_col = x_col + length * p_col
             r_col = r_col - length * q_col
             r_row = r_row - length * q_row
-            fresh = quad(r_col, r_row)
+            fresh = quad(gram, r_col, r_row)
             ratio = fresh / norm
             p_col = r_col + ratio * p_col
             p_row = r_row + ratio * p_row
@@ -356,7 +373,7 @@
                 pltpu.VMEM((2, LANES), f32),
                 pltpu.VMEM((2, count, 2, LANES), f32),
                 pltpu.VMEM((2, bz, hy, bx), f32),
-                dma((2,)), dma((2,)), dma((2, 3)), dma((2, 3)),
+                dma((2, 2)), dma((2, 2)), dma((2, 2, 3)), dma((2, 2, 3)),
                 dma, dma((2,)), dma((2,)), dma((2,)), dma((2,)),
             ],
             compiler_params=pltpu.CompilerParams(has_side_effects=True),

time: 103 us -> 88.2 us (0.86)
  Pallas kernels: 99.8 us -> 85.2 us
    pallas_call x1, Pallas kernels: 99.8 us -> 85.2 us  [body(): pl.pallas_call(lambda *refs: kernel(nz, ny, nx, *refs), out_shape=(jax.Sh...]
where the time goes in v2:
time: 88.2 us; the launch traced here: 88 us
  Pallas kernels  85.2 us (97%)
  local copies, waits for them, and re-layouts  2.14 us (2%)
    pallas_call x1, Pallas kernels, body(): pl.pallas_call(lambda *refs: kernel(nz, ny, nx, *refs), out_shape=(jax.Sh...  85.2 us
    unnamed x4, local copies, waits for them, and re-layouts  2.14 us

profile of v2, /device:TPU:0, one launch (start us, length us, event | category | flops | bytes accessed | tf_op | source)
XLA Modules:
  0.0 88.0 jit_solution(2036130585993644463)
XLA Ops:
  0.6 85.2 %shard_map.41 = (f32[8,16,128]{2,1,0:T(8,128)}, f32[8,16,128]{2,1,0:T(8,128)}) custom-call(f32[8,16,128]{2,1,0:T(8,128)} %refs_0_.1, f32[8,16,128]{2,1,0:T(8,128)} %refs_1_.1), custom_call_target="tpu_custom_call" | custom-call | tf_op jit(solution)/shard_map/pallas_call | solution.py:360
  85.8 0.0 copy-start
  85.8 1.5 %copy.6 = f32[8,16,128]{2,1,0:T(8,128)} copy(f32[8,16,128]{2,1,0:T(8,128)} %get-tuple-element.4) | data formatting | bytes 131072
  87.3 0.0 copy-done
  87.3 0.6 copy.7
Async XLA Ops:
  85.8 1.5 %copy-start = (f32[8,16,128]{2,1,0:T(8,128)S(1)}, f32[8,16,128]{2,1,0:T(8,128)}, u32[]{:S(2)}) copy-start(f32[8,16,128]{2,1,0:T(8,128)} %get-tuple-element.5) | copy-start | bytes 196612

commit v3 on v2

--- a/solution.py
+++ b/solution.py
@@ -38,7 +38,7 @@
 
 
 def kernel(nz, ny, nx, rhs_ref, diag_ref, sol_out, res_out,
-           fields, p_chain, r_chain, scale2, weight, total, pairs, g_send, g_recv, final,
+           fields, p_chain, r_chain, scale2, weight, total, pairs, g_send, g_recv, final, kept,
            z_send, z_recv, y_send, y_recv, g_ssem, g_rsem, swap_send, swap_recv, own_sem):
     bz, by, bx = rhs_ref.shape
     hy = by // 2
@@ -122,18 +122,17 @@
             send_sem=y_send.at[k, side, part], recv_sem=y_recv.at[k, 1 - side, part],
             device_id=y_dev[side], device_id_type=MESH)
 
-    def exchange(shallow):
-        items = ((1, S, 0), (shallow, S - 1, 1))
-        for item in items:
-            for side in range(2):
-                @pl.when(has_z[side])
-                def _():
-                    z_copy(item, side).start()
-        for item in items:
-            for side in range(2):
-                @pl.when(has_y[side])
-                def _():
-                    y_copy(item, side, 0).start()
+    def start(item):
+        for side in range(2):
+            @pl.when(has_z[side])
+            def _():
+                z_copy(item, side).start()
+        for side in range(2):
+            @pl.when(has_y[side])
+            def _():
+                y_copy(item, side, 0).start()
+
+    def finish(items):
         for item in items:
             for z_side in range(2):
                 @pl.when(has_z[z_side])
@@ -159,7 +158,9 @@
                             y_copy(item, side, 1 + z_side).wait_send()
                             y_copy(item, 1 - side, 1 + z_side).wait_recv()
 
-    exchange(2)
+    start((1, S, 0))
+    start((2, S - 1, 1))
+    finish(((1, S, 0), (2, S - 1, 1)))
     all_rows = slice(first - ROWS, first + hy + ROWS)
 
     def prepare(plane, c):
@@ -274,6 +275,8 @@
                 device_id=(peer // (ny * nx), (peer // nx) % ny, peer % nx), device_id_type=MESH).start()
             return c
         lax.fori_loop(0, count - 1, send, 0, unroll=4)
+        for k in range(2):
+            kept[k] = fields[1 - k, mid_z, :, mid_y, :]
         everything = g_recv.at[slot]
         pltpu.make_async_copy(everything, everything, g_rsem.at[slot]).wait()
         most = g_recv.at[slot, 0:count - 1]
@@ -314,22 +317,30 @@
             return [jnp.broadcast_to(col[i:i + 1, :], (hy, LANES)) for i in range(COLS)]
 
         xw, rw, pw = weights(x_col), weights(r_col), weights(p_col)
-        for z in range(bz):
-            for h in range(halves):
-                vs = [b[S + z, h, mid_y, :] for b in basis]
-
-                def mix(w):
-                    out = w[0] * vs[0]
-                    for a, b in zip(w[1:], vs[1:]):
-                        out = out + a * b
-                    return out
-                total[0, z, h] = total[0, z, h] + mix(xw)
-                fields[0, S + z, h, mid_y, :] = mix(rw)
-                fields[1, S + z, h, mid_y, :] = mix(pw)
+        cells = [(z, h) for z in range(bz) for h in range(halves)]
+
+        def mix(w, z, h):
+            vs = [kept[0, z, h]] + [b[S + z, h, mid_y, :] for b in p_at[1:]]
+            vs += [kept[1, z, h]] + [b[S + z, h, mid_y, :] for b in r_at[1:]]
+            out = w[0] * vs[0]
+            for a, b in zip(w[1:], vs[1:]):
+                out = out + a * b
+            return out
+
+        items = ((1, S, 0), (0, S - 1, 1))
+        for item, w in zip(items, (pw, rw)):
+            for z, h in cells:
+                fields[item[0], S + z, h, mid_y, :] = mix(w, z, h)
+
+            @pl.when(t < OUTER - 1)
+            def _():
+                start(item)
+        for z, h in cells:
+            total[0, z, h] = total[0, z, h] + mix(xw, z, h)
 
         @pl.when(t < OUTER - 1)
         def _():
-            exchange(0)
+            finish(items)
         return carry
 
     lax.fori_loop(0, OUTER, outer, 0)
@@ -373,6 +384,7 @@
                 pltpu.VMEM((2, LANES), f32),
                 pltpu.VMEM((2, count, 2, LANES), f32),
                 pltpu.VMEM((2, bz, hy, bx), f32),
+                pltpu.VMEM((2, bz, nx, hy, bx), f32),
                 dma((2, 2)), dma((2, 2)), dma((2, 2, 3)), dma((2, 2, 3)),
                 dma, dma((2,)), dma((2,)), dma((2,)), dma((2,)),
             ],

time: 88.2 us -> 88.2 us (level)
  no operation moved by 1% of the time
where the time goes in v3:
time: 88.2 us; the launch traced here: 88 us
  Pallas kernels  85.2 us (97%)
  local copies, waits for them, and re-layouts  2.14 us (2%)
    pallas_call x1, Pallas kernels, body(): pl.pallas_call(lambda *refs: kernel(nz, ny, nx, *refs), out_shape=(jax.Sh...  85.2 us
    unnamed x4, local copies, waits for them, and re-layouts  2.14 us

profile of v3, /device:TPU:0, one launch (start us, length us, event | category | flops | bytes accessed | tf_op | source)
XLA Modules:
  0.0 88.0 jit_solution(2811099400303561031)
XLA Ops:
  0.6 85.2 %shard_map.41 = (f32[8,16,128]{2,1,0:T(8,128)}, f32[8,16,128]{2,1,0:T(8,128)}) custom-call(f32[8,16,128]{2,1,0:T(8,128)} %refs_0_.1, f32[8,16,128]{2,1,0:T(8,128)} %refs_1_.1), custom_call_target="tpu_custom_call" | custom-call | tf_op jit(solution)/shard_map/pallas_call | solution.py:371
  85.8 0.0 copy-start
  85.8 1.5 %copy.6 = f32[8,16,128]{2,1,0:T(8,128)} copy(f32[8,16,128]{2,1,0:T(8,128)} %get-tuple-element.4) | data formatting | bytes 131072
  87.3 0.0 copy-done
  87.4 0.6 copy.7
Async XLA Ops:
  85.8 1.5 %copy-start = (f32[8,16,128]{2,1,0:T(8,128)S(1)}, f32[8,16,128]{2,1,0:T(8,128)}, u32[]{:S(2)}) copy-start(f32[8,16,128]{2,1,0:T(8,128)} %get-tuple-element.5) | copy-start | bytes 196612
